TPU v7x, 32 devices: a whole 2x2x4 slice. The times are simulated.
32 devices in a mesh: dp: 8 (over y, x, core), seq: 4 (over z).
Axes of the slice: x: 2, y: 2, z: 4, core: 2. Of those that a mesh axis runs over, the one named last changes fastest.
Arguments:
- img_q_raw: bfloat16 [8, 512, 1536], P('dp', 'seq'), may hold values from -12 to 12
- img_k_raw: bfloat16 [8, 512, 1536], P('dp', 'seq'), may hold values from -6 to 6
- img_v: bfloat16 [8, 512, 1536], P('dp', 'seq'), may hold values from -6 to 6
- img_dout: bfloat16 [8, 512, 1536], P('dp', 'seq'), may hold values from -6 to 6
- txt_q_raw: bfloat16 [8, 64, 1536], P('dp', 'seq'), may hold values from -6 to 6
- txt_k_raw: bfloat16 [8, 64, 1536], P('dp'), may hold values from -6 to 6
- txt_v: bfloat16 [8, 64, 1536], P('dp'), may hold values from -6 to 6
- txt_dout: bfloat16 [8, 64, 1536], P('dp', 'seq'), may hold values from -6 to 6
- q_gain: float32 [128], replicated, may hold values from 0.6 to 3.8
- k_gain: float32 [128], replicated, may hold values from 0.6 to 3.8
Outputs:
- img_dq: bfloat16 [8, 512, 1536], P('dp', 'seq')
- img_dk: bfloat16 [8, 512, 1536], P('dp', 'seq')
- img_dv: bfloat16 [8, 512, 1536], P('dp', 'seq')
- txt_dq: bfloat16 [8, 64, 1536], P('dp', 'seq')
- txt_dk: bfloat16 [8, 64, 1536], P('dp', 'seq')
- txt_dv: bfloat16 [8, 64, 1536], P('dp', 'seq')
- q_gain_grad: float32 [128], replicated
- k_gain_grad: float32 [128], replicated
All inputs are finite; a program needn't handle non-finite values.
Results may differ from a plain program's by a relative error of at most 0.012.
The roundings to bfloat16 on the way count: a program that leaves them out, or rounds other values in their place, can miss the bound.
Values may be sent and summed in bfloat16 or wider, within the bound.
A program may use at most 64 MiB of HBM per device.

v0:
```python
import jax
import jax.numpy as jnp
from jax import lax
from jax.sharding import PartitionSpec as P

HEAD_DIM = 128
epsilon = 1e-06


def normalize(source, norm_gain):
    values = source.astype(jnp.float32)
    inverse = lax.rsqrt(jnp.mean(values * values, axis=-1, keepdims=True) + epsilon)
    return values * inverse * norm_gain


def norm_backward(source, norm_gain, upstream):
    values = source.astype(jnp.float32)
    result_value, pullback = jax.vjp(normalize, values, norm_gain)
    return pullback(upstream)


def group_back(operands):
    query_b, key_b, value_all, dout_blocks = operands
    score_scale = query_b.shape[-1] ** (-0.5)
    scores = (
        jnp.einsum("nqhd,khd->nhqk", query_b, key_b, preferred_element_type=jnp.float32)
        * score_scale
    )
    row_max = jnp.max(scores, axis=-1, keepdims=True)
    shifted = scores - row_max
    log_total = jnp.log(jnp.sum(jnp.exp(shifted), axis=-1, keepdims=True))
    prob_full = jnp.exp(shifted - log_total)
    probs_b = prob_full.astype(jnp.bfloat16)
    output_b = jnp.einsum(
        "nhqk,khd->nqhd", probs_b, value_all, preferred_element_type=jnp.float32
    ).astype(jnp.bfloat16)
    output_b = lax.optimization_barrier(output_b)
    dprob = jnp.einsum("nqhd,khd->nhqk", dout_blocks, value_all, preferred_element_type=jnp.float32)
    row_delta = jnp.sum(dout_blocks.astype(jnp.float32) * output_b.astype(jnp.float32), axis=-1)
    row_delta = jnp.transpose(row_delta, (0, 2, 1))[..., None]
    dscore_b = (prob_full * (dprob - row_delta) * score_scale).astype(jnp.bfloat16)
    dquery = jnp.einsum("nhqk,khd->nqhd", dscore_b, key_b, preferred_element_type=jnp.float32)
    key_terms = jnp.einsum("nhqk,nqhd->nkhd", dscore_b, query_b, preferred_element_type=jnp.float32)
    value_terms = jnp.einsum(
        "nhqk,nqhd->nkhd", probs_b, dout_blocks, preferred_element_type=jnp.float32
    )
    return (dquery, key_terms, value_terms)


def forward_back(query_b, key_b, value_all, dout_blocks):
    block_count, query_rows, heads_here, feature_count = query_b.shape
    key_rows = key_b.shape[0]
    group_count = heads_here // heads_here

    def split_rows(source):
        return jnp.moveaxis(
            source.reshape(block_count, query_rows, group_count, heads_here, feature_count), 2, 0
        )

    def split_keys(source):
        return jnp.moveaxis(source.reshape(key_rows, group_count, heads_here, feature_count), 1, 0)

    dquery_g, key_g, value_g = lax.map(
        group_back,
        (split_rows(query_b), split_keys(key_b), split_keys(value_all), split_rows(dout_blocks)),
    )
    dquery = jnp.moveaxis(dquery_g, 0, 2).reshape(
        block_count, query_rows, heads_here, feature_count
    )
    key_terms = jnp.moveaxis(key_g, 0, 2).reshape(block_count, key_rows, heads_here, feature_count)
    value_terms = jnp.moveaxis(value_g, 0, 2).reshape(
        block_count, key_rows, heads_here, feature_count
    )
    return (dquery, key_terms, value_terms)


def local(
    img_q_raw, img_k_raw, img_v, img_dout, txt_q_raw, txt_k_raw, txt_v, txt_dout, q_gain, k_gain
):
    seq_count = lax.axis_size("seq")
    my_index = lax.axis_index("seq")
    image_q = img_q_raw[0]
    image_k = img_k_raw[0]
    image_v = img_v[0]
    image_d = img_dout[0]
    text_q = txt_q_raw[0]
    text_k = txt_k_raw[0]
    text_v = txt_v[0]
    text_d = txt_dout[0]
    lane_width = image_q.shape[1]
    head_count = lane_width // HEAD_DIM
    img_rows = image_q.shape[0]
    text_rows = text_q.shape[0]
    text_all = text_k.shape[0]
    image_total = img_rows * seq_count
    exchanged = (
        lax.all_to_all(image_q, "seq", split_axis=1, concat_axis=0, tiled=True),
        lax.all_to_all(image_k, "seq", split_axis=1, concat_axis=0, tiled=True),
        lax.all_to_all(image_v, "seq", split_axis=1, concat_axis=0, tiled=True),
        lax.all_to_all(image_d, "seq", split_axis=1, concat_axis=0, tiled=True),
        lax.all_to_all(text_q, "seq", split_axis=1, concat_axis=0, tiled=True),
        lax.all_to_all(text_d, "seq", split_axis=1, concat_axis=0, tiled=True),
    )
    moved_iq, moved_ik, moved_iv, moved_id, moved_tq, moved_td = exchanged
    local_heads = head_count // seq_count
    head_lanes = local_heads * HEAD_DIM
    key_text = lax.dynamic_slice_in_dim(text_k, my_index * head_lanes, head_lanes, 1)
    value_text = lax.dynamic_slice_in_dim(text_v, my_index * head_lanes, head_lanes, 1)
    query_src = jnp.concatenate(
        [
            moved_iq.reshape(seq_count, img_rows, local_heads, HEAD_DIM),
            moved_tq.reshape(seq_count, text_rows, local_heads, HEAD_DIM),
        ],
        axis=1,
    )
    dout_blocks = jnp.concatenate(
        [
            moved_id.reshape(seq_count, img_rows, local_heads, HEAD_DIM),
            moved_td.reshape(seq_count, text_rows, local_heads, HEAD_DIM),
        ],
        axis=1,
    )
    key_src = jnp.concatenate([moved_ik, key_text], axis=0).reshape(
        image_total + text_all, local_heads, HEAD_DIM
    )
    value_all = jnp.concatenate([moved_iv, value_text], axis=0).reshape(
        image_total + text_all, local_heads, HEAD_DIM
    )
    query_b = normalize(query_src, q_gain).astype(jnp.bfloat16)
    key_b = normalize(key_src, k_gain).astype(jnp.bfloat16)
    dquery, key_f, value_f = forward_back(query_b, key_b, value_all, dout_blocks)
    key_terms = key_f.astype(jnp.bfloat16)
    value_terms = value_f.astype(jnp.bfloat16)
    key_terms, value_terms = lax.optimization_barrier((key_terms, value_terms))
    dkey = jnp.sum(key_terms.astype(jnp.float32), axis=0)
    dvalue = jnp.sum(value_terms.astype(jnp.float32), axis=0)
    dquery_src, dq_gain = norm_backward(query_src, q_gain, dquery)
    dkey_src, dk_gain = norm_backward(key_src, k_gain, dkey)
    dq_b = dquery_src.astype(jnp.bfloat16)
    dk_b = dkey_src.reshape(image_total + text_all, head_lanes).astype(jnp.bfloat16)
    dv_b = dvalue.reshape(image_total + text_all, head_lanes).astype(jnp.bfloat16)
    returned = (
        dq_b[:, :img_rows].reshape(image_total, head_lanes),
        dk_b[:image_total],
        dv_b[:image_total],
        dq_b[:, img_rows:].reshape(text_all, head_lanes),
        dk_b[image_total:],
        dv_b[image_total:],
    )
    grad_iq, grad_ik, grad_iv, grad_tq, grad_tk, grad_tv = (
        lax.all_to_all(returned[0], "seq", split_axis=0, concat_axis=1, tiled=True),
        lax.all_to_all(returned[1], "seq", split_axis=0, concat_axis=1, tiled=True),
        lax.all_to_all(returned[2], "seq", split_axis=0, concat_axis=1, tiled=True),
        lax.all_to_all(returned[3], "seq", split_axis=0, concat_axis=1, tiled=True),
        lax.all_to_all(returned[4], "seq", split_axis=0, concat_axis=1, tiled=True),
        lax.all_to_all(returned[5], "seq", split_axis=0, concat_axis=1, tiled=True),
    )
    gain_q, gain_k = lax.psum((dq_gain, dk_gain), ("dp", "seq"))
    return (
        grad_iq[None],
        grad_ik[None],
        grad_iv[None],
        grad_tq[None],
        grad_tk[None],
        grad_tv[None],
        gain_q,
        gain_k,
    )


def solution(mesh):
    return jax.shard_map(
        local,
        mesh=mesh,
        in_specs=(
            P("dp", "seq", None),
            P("dp", "seq", None),
            P("dp", "seq", None),
            P("dp", "seq", None),
            P("dp", "seq", None),
            P("dp", None, None),
            P("dp", None, None),
            P("dp", "seq", None),
            P(),
            P(),
        ),
        out_specs=(
            P("dp", "seq", None),
            P("dp", "seq", None),
            P("dp", "seq", None),
            P("dp", "seq", None),
            P("dp", "seq", None),
            P("dp", "seq", None),
            P(),
            P(),
        ),
        check_vma=False,
    )
```

profile of v0, /device:TPU:0, one launch (start us, length us, event | category | flops | bytes accessed | tf_op | source)
XLA Modules:
  0.0 206.6 jit_solution(5955745471128264303)
XLA Ops:
  2.2 6.3 %all-to-all-start.2 = ((bf16[16,4,384]{2,0,1:T(8,128)(2,1)}), bf16[16,4,384]{2,0,1:T(8,128)(2,1)S(1)}, u32[]{:S(2)}, u32[]{:S(2)}) async-start(bf16[16,4,384]{2,0,1:T(8,128)(2,1)} %copy.91), calls=%async_computation.2 | async-start | bytes 98304 | tf_op jit(solution)/shard_map/all_to_all | solution.py:101
  9.9 4.3 %all-to-all-done.2 = bf16[16,4,384]{2,0,1:T(8,128)(2,1)S(1)} async-done(((bf16[16,4,384]{2,0,1:T(8,128)(2,1)}), bf16[16,4,384]{2,0,1:T(8,128)(2,1)S(1)}, u32[]{:S(2)}, u32[]{:S(2)}) %all-to-all-start.2) | async-done | bytes 49184 | tf_op jit(solution)/shard_map/all_to_all | solution.py:101
  14.2 3.3 %all-to-all-start.5 = ((bf16[16,4,384]{2,0,1:T(8,128)(2,1)}), bf16[16,4,384]{2,0,1:T(8,128)(2,1)S(1)}, u32[]{:S(2)}, u32[]{:S(2)}) async-start(bf16[16,4,384]{2,0,1:T(8,128)(2,1)} %copy.99), calls=%async_computation.5 | async-start | bytes 98304 | tf_op jit(solution)/shard_map/all_to_all | solution.py:102
  17.5 1.9 copy.86
  19.4 3.8 %all-to-all-done.5 = bf16[16,4,384]{2,0,1:T(8,128)(2,1)S(1)} async-done(((bf16[16,4,384]{2,0,1:T(8,128)(2,1)}), bf16[16,4,384]{2,0,1:T(8,128)(2,1)S(1)}, u32[]{:S(2)}, u32[]{:S(2)}) %all-to-all-start.5) | async-done | bytes 49184 | tf_op jit(solution)/shard_map/all_to_all | solution.py:102
  23.1 3.5 %all-to-all-start = ((bf16[128,4,384]{0,2,1:T(8,128)(2,1)}), bf16[128,4,384]{0,2,1:T(8,128)(2,1)S(1)}, u32[]{:S(2)}, u32[]{:S(2)}) async-start(bf16[128,4,384]{0,2,1:T(8,128)(2,1)} %bitcast), calls=%async_computation | async-start | bytes 786432 | tf_op jit(solution)/shard_map/all_to_all | solution.py:98
  28.3 1.9 copy.90
  30.8 1.9 copy.94
  33.7 2.3 %all-to-all-done = bf16[128,4,384]{0,2,1:T(8,128)(2,1)S(1)} async-done(((bf16[128,4,384]{0,2,1:T(8,128)(2,1)}), bf16[128,4,384]{0,2,1:T(8,128)(2,1)S(1)}, u32[]{:S(2)}, u32[]{:S(2)}) %all-to-all-start) | async-done | bytes 393248 | tf_op jit(solution)/shard_map/all_to_all | solution.py:98
  36.0 3.5 %all-to-all-start.1 = ((bf16[128,4,384]{0,2,1:T(8,128)(2,1)}), bf16[128,4,384]{0,2,1:T(8,128)(2,1)S(1)}, u32[]{:S(2)}, u32[]{:S(2)}) async-start(bf16[128,4,384]{0,2,1:T(8,128)(2,1)} %bitcast.4), calls=%async_computation.1 | async-start | bytes 786432 | tf_op jit(solution)/shard_map/all_to_all | solution.py:97
  40.2 8.6 %all-to-all-done.1 = bf16[128,4,384]{0,2,1:T(8,128)(2,1)S(1)} async-done(((bf16[128,4,384]{0,2,1:T(8,128)(2,1)}), bf16[128,4,384]{0,2,1:T(8,128)(2,1)S(1)}, u32[]{:S(2)}, u32[]{:S(2)}) %all-to-all-start.1) | async-done | bytes 393248 | tf_op jit(solution)/shard_map/all_to_all | solution.py:97
  48.7 3.5 %all-to-all-start.3 = ((bf16[128,4,384]{0,2,1:T(8,128)(2,1)}), bf16[128,4,384]{0,2,1:T(8,128)(2,1)S(1)}, u32[]{:S(2)}, u32[]{:S(2)}) async-start(bf16[128,4,384]{0,2,1:T(8,128)(2,1)} %bitcast.12), calls=%async_computation.3 | async-start | bytes 786432 | tf_op jit(solution)/shard_map/all_to_all | solution.py:99
  54.5 2.9 %fusion.39 = f32[3,576,576]{1,2,0} fusion(bf16[3,128,576]{1,2,0:T(8,128)(2,1)S(1)} %bitcast.111, f32[128]{0:T(128)S(1)} %copy-done.15, f32[576,3]{0,1:T(4,128)S(1)} %fusion.43, bf16[64,3,128]{2,0,1:T(8,128)(2,1)S(1)} %copy.89, bf16[512,3,128]{2,0,1:T(8,128)(2,1)S(1)} %copy.88), kind=kOutput, calls=%fused_computation.57 | convolution fusion | flops 256352256 | bytes 4873472
  57.3 4.2 %all-to-all-done.3 = bf16[128,4,384]{0,2,1:T(8,128)(2,1)S(1)} async-done(((bf16[128,4,384]{0,2,1:T(8,128)(2,1)}), bf16[128,4,384]{0,2,1:T(8,128)(2,1)S(1)}, u32[]{:S(2)}, u32[]{:S(2)}) %all-to-all-start.3) | async-done | bytes 393248 | tf_op jit(solution)/shard_map/all_to_all | solution.py:99
  61.5 3.6 %all-to-all-start.4 = ((bf16[128,4,384]{0,2,1:T(8,128)(2,1)}), bf16[128,4,384]{0,2,1:T(8,128)(2,1)S(1)}, u32[]{:S(2)}, u32[]{:S(2)}) async-start(bf16[128,4,384]{0,2,1:T(8,128)(2,1)} %bitcast.14), calls=%async_computation.4 | async-start | bytes 786432 | tf_op jit(solution)/shard_map/all_to_all | solution.py:100
  65.2 6.4 %bitcast_subtract_fusion = f32[4,3,144,576]{3,2,0,1:T(8,128)} fusion(f32[3,576,4,144]{1,3,2,0:T(8,128)} %bitcast.107), kind=kOutput, calls=%fused_computation.5 | output fusion | flops 2988287 | bytes 7962624 | tf_op jit(solution)/shard_map/while/body/eval_jaxpr/sub | solution.py:30
  72.9 7.0 %fusion.47 = (bf16[4,3,144,576]{3,2,0,1:T(8,128)(2,1)S(1)}, f32[4,3,144,576]{3,2,0,1:T(8,128)}) fusion(f32[4,3,144,576]{3,2,0,1:T(8,128)} %bitcast_subtract_fusion), kind=kOutput, calls=%fused_computation.75 | output fusion | flops 1992959 | bytes 9953280 | tf_op jit(solution)/shard_map/while/body/eval_jaxpr/reduce_sum | solution.py:31
  82.0 2.5 %convert_bitcast_fusion = bf16[4,576,3,128]{3,1,2,0:T(8,128)(2,1)} fusion(bf16[4,3,144,576]{3,2,0,1:T(8,128)(2,1)S(1)} %get-tuple-element.66, bf16[4,16,3,128]{3,1,0,2:T(8,128)(2,1)S(1)} %copy_bitcast_fusion.1, bf16[4,128,3,128]{3,1,0,2:T(8,128)(2,1)S(1)} %copy.100), kind=kOutput, calls=%fused_computation.17 | convolution fusion | flops 256573440 | bytes 4202496 | tf_op jit(solution)/shard_map/while/body/eval_jaxpr/nhqk,nqhd->nkhd/dot_general | solution.py:44
  88.8 2.5 %fusion.26 = (f32[128]{0:T(128)}, f32[4,144,3]{1,0,2:T(4,128)}, f32[4,144,3,128]{3,1,0,2:T(8,128)}) fusion(f32[4,144,3]{1,0,2:T(4,128)S(1)} %copy-done.11, bf16[4,16,3,128]{3,1,0,2:T(8,128)(2,1)S(1)} %copy_bitcast_fusion.2, bf16[4,128,3,128]{3,1,0,2:T(8,128)(2,1)S(1)} %copy.92, f32[128]{0:T(128)S(1)} %copy-done.18, ...), kind=kOutput, calls=%fused_computation.40 | convolution fusion | flops 258562240 | bytes 3782400 | tf_op jit(solution)/shard_map/while/body/eval_jaxpr/nhqk,khd->nqhd/dot_general | solution.py:42
  98.4 4.9 %all-to-all-start.10 = ((bf16[4,16,384]{2,1,0:T(8,128)(2,1)}), bf16[4,16,384]{2,1,0:T(8,128)(2,1)S(1)}, u32[]{:S(2)}, u32[]{:S(2)}) async-start(bf16[4,16,384]{2,1,0:T(8,128)(2,1)} %bitcast.44), calls=%async_computation.10 | async-start | bytes 98304 | tf_op jit(solution)/shard_map/all_to_all | solution.py:155
  104.0 1.7 fusion.31
  107.0 2.0 all-to-all-done.10
  109.0 3.5 %all-to-all-start.11 = ((bf16[4,16,384]{2,1,0:T(8,128)(2,1)}), bf16[4,16,384]{2,1,0:T(8,128)(2,1)S(1)}, u32[]{:S(2)}, u32[]{:S(2)}) async-start(bf16[4,16,384]{2,1,0:T(8,128)(2,1)} %all_to_all.177), calls=%async_computation.11 | async-start | bytes 98304 | tf_op jit(solution)/shard_map/all_to_all | solution.py:156
  113.2 5.0 %all-to-all-done.11 = bf16[4,16,384]{2,1,0:T(8,128)(2,1)S(1)} async-done(((bf16[4,16,384]{2,1,0:T(8,128)(2,1)}), bf16[4,16,384]{2,1,0:T(8,128)(2,1)S(1)}, u32[]{:S(2)}, u32[]{:S(2)}) %all-to-all-start.11) | async-done | bytes 49184 | tf_op jit(solution)/shard_map/all_to_all | solution.py:156
  118.2 3.3 %all-to-all-start.9 = ((bf16[4,16,384]{2,1,0:T(8,128)(2,1)}), bf16[4,16,384]{2,1,0:T(8,128)(2,1)S(1)}, u32[]{:S(2)}, u32[]{:S(2)}) async-start(bf16[4,16,384]{2,1,0:T(8,128)(2,1)} %copy_bitcast_fusion), calls=%async_computation.9 | async-start | bytes 98304 | tf_op jit(solution)/shard_map/all_to_all | solution.py:154
  122.4 4.8 %all-to-all-done.9 = bf16[4,16,384]{2,1,0:T(8,128)(2,1)S(1)} async-done(((bf16[4,16,384]{2,1,0:T(8,128)(2,1)}), bf16[4,16,384]{2,1,0:T(8,128)(2,1)S(1)}, u32[]{:S(2)}, u32[]{:S(2)}) %all-to-all-start.9) | async-done | bytes 49184 | tf_op jit(solution)/shard_map/all_to_all | solution.py:154
  127.2 3.5 %all-to-all-start.7 = ((bf16[4,128,384]{2,1,0:T(8,128)(2,1)}), bf16[4,128,384]{2,1,0:T(8,128)(2,1)S(1)}, u32[]{:S(2)}, u32[]{:S(2)}) async-start(bf16[4,128,384]{2,1,0:T(8,128)(2,1)} %bitcast.38), calls=%async_computation.7 | async-start | bytes 786432 | tf_op jit(solution)/shard_map/all_to_all | solution.py:152
  131.8 7.7 %all-to-all-done.7 = bf16[4,128,384]{2,1,0:T(8,128)(2,1)S(1)} async-done(((bf16[4,128,384]{2,1,0:T(8,128)(2,1)}), bf16[4,128,384]{2,1,0:T(8,128)(2,1)S(1)}, u32[]{:S(2)}, u32[]{:S(2)}) %all-to-all-start.7) | async-done | bytes 393248 | tf_op jit(solution)/shard_map/all_to_all | solution.py:152
  139.6 5.6 %all-to-all-start.8 = ((bf16[4,128,384]{1,2,0:T(8,128)(2,1)}), bf16[4,128,384]{1,2,0:T(8,128)(2,1)S(1)}, u32[]{:S(2)}, u32[]{:S(2)}) async-start(bf16[4,128,384]{1,2,0:T(8,128)(2,1)} %copy.115), calls=%async_computation.8 | async-start | bytes 786432 | tf_op jit(solution)/shard_map/all_to_all | solution.py:153
  146.1 11.2 %all-to-all-done.8 = bf16[4,128,384]{1,2,0:T(8,128)(2,1)S(1)} async-done(((bf16[4,128,384]{1,2,0:T(8,128)(2,1)}), bf16[4,128,384]{1,2,0:T(8,128)(2,1)S(1)}, u32[]{:S(2)}, u32[]{:S(2)}) %all-to-all-start.8) | async-done | bytes 393248 | tf_op jit(solution)/shard_map/all_to_all | solution.py:153
  157.4 3.5 %all-to-all-start.6 = ((bf16[4,128,384]{1,2,0:T(8,128)(2,1)}), bf16[4,128,384]{1,2,0:T(8,128)(2,1)S(1)}, u32[]{:S(2)}, u32[]{:S(2)}) async-start(bf16[4,128,384]{1,2,0:T(8,128)(2,1)} %bitcast.27), calls=%async_computation.6 | async-start | bytes 786432 | tf_op jit(solution)/shard_map/all_to_all | solution.py:151
  160.8 40.7 %all-reduce = (f32[128]{0:T(128)}, f32[128]{0:T(128)}) all-reduce(f32[128]{0:T(128)S(1)} %copy-done.20, f32[128]{0:T(128)S(1)} %copy-done.19), channel_id=1, replica_groups=mesh['dp'=8,'seq'=4] {'dp','seq'}, use_global_device_ids=true, to_apply=%region_10.11 | all-reduce | flops 256 | bytes 2048 | tf_op jit(solution)/shard_map/psum | solution.py:158
  (115 shorter events, 34.3 us)
Async XLA Ops:
  0.6 32.1 %copy-start.7 = (bf16[1,128,1536]{2,1,0:T(8,128)(2,1)S(1)}, bf16[1,128,1536]{2,1,0:T(8,128)(2,1)}, u32[]{:S(2)}) copy-start(bf16[1,128,1536]{2,1,0:T(8,128)(2,1)} %param.13) | copy-start | bytes 1179652
  0.6 38.8 %copy-start.15 = (f32[128]{0:T(128)S(1)}, f32[128]{0:T(128)}, u32[]{:S(2)}) copy-start(f32[128]{0:T(128)} %param.19) | copy-start | bytes 1540
  2.2 12.0 %all-to-all-start.2 = ((bf16[16,4,384]{2,0,1:T(8,128)(2,1)}), bf16[16,4,384]{2,0,1:T(8,128)(2,1)S(1)}, u32[]{:S(2)}, u32[]{:S(2)}) async-start(bf16[16,4,384]{2,0,1:T(8,128)(2,1)} %copy.91), calls=%async_computation.2 | async-start | bytes 98304 | tf_op jit(solution)/shard_map/all_to_all | solution.py:101
  14.2 8.9 %all-to-all-start.5 = ((bf16[16,4,384]{2,0,1:T(8,128)(2,1)}), bf16[16,4,384]{2,0,1:T(8,128)(2,1)S(1)}, u32[]{:S(2)}, u32[]{:S(2)}) async-start(bf16[16,4,384]{2,0,1:T(8,128)(2,1)} %copy.99), calls=%async_computation.5 | async-start | bytes 98304 | tf_op jit(solution)/shard_map/all_to_all | solution.py:102
  23.1 12.8 %all-to-all-start = ((bf16[128,4,384]{0,2,1:T(8,128)(2,1)}), bf16[128,4,384]{0,2,1:T(8,128)(2,1)S(1)}, u32[]{:S(2)}, u32[]{:S(2)}) async-start(bf16[128,4,384]{0,2,1:T(8,128)(2,1)} %bitcast), calls=%async_computation | async-start | bytes 786432 | tf_op jit(solution)/shard_map/all_to_all | solution.py:98
  27.5 25.9 %copy-start.17 = (f32[128]{0:T(128)S(1)}, f32[128]{0:T(128)}, u32[]{:S(2)}) copy-start(f32[128]{0:T(128)} %param.18) | copy-start | bytes 1540
  36.0 16.3 %copy-start.3 = (bf16[128,4,384]{0,2,1:T(8,128)(2,1)}, bf16[128,4,384]{0,2,1:T(8,128)(2,1)S(1)}, u32[]{:S(2)}) copy-start(bf16[128,4,384]{0,2,1:T(8,128)(2,1)S(1)} %all-to-all-done) | copy-start | bytes 1179652
  36.0 12.8 %all-to-all-start.1 = ((bf16[128,4,384]{0,2,1:T(8,128)(2,1)}), bf16[128,4,384]{0,2,1:T(8,128)(2,1)S(1)}, u32[]{:S(2)}, u32[]{:S(2)}) async-start(bf16[128,4,384]{0,2,1:T(8,128)(2,1)} %bitcast.4), calls=%async_computation.1 | async-start | bytes 786432 | tf_op jit(solution)/shard_map/all_to_all | solution.py:97
  48.7 12.8 %all-to-all-start.3 = ((bf16[128,4,384]{0,2,1:T(8,128)(2,1)}), bf16[128,4,384]{0,2,1:T(8,128)(2,1)S(1)}, u32[]{:S(2)}, u32[]{:S(2)}) async-start(bf16[128,4,384]{0,2,1:T(8,128)(2,1)} %bitcast.12), calls=%async_computation.3 | async-start | bytes 786432 | tf_op jit(solution)/shard_map/all_to_all | solution.py:99
  53.0 18.6 %copy-start.12 = (f32[4,144,3]{1,0,2:T(4,128)}, f32[4,144,3]{1,0,2:T(4,128)S(1)}, u32[]{:S(2)}) copy-start(f32[4,144,3]{1,0,2:T(4,128)S(1)} %fusion.32) | copy-start | bytes 20740
  53.0 18.6 %copy-start.10 = (f32[4,144,3]{1,0,2:T(4,128)}, f32[4,144,3]{1,0,2:T(4,128)S(1)}, u32[]{:S(2)}) copy-start(f32[4,144,3]{1,0,2:T(4,128)S(1)} %fusion.42) | copy-start | bytes 20740
  53.4 18.2 %copy-start.13 = (f32[576,3]{0,1:T(4,128)}, f32[576,3]{0,1:T(4,128)S(1)}, u32[]{:S(2)}) copy-start(f32[576,3]{0,1:T(4,128)S(1)} %fusion.29) | copy-start | bytes 20740
  61.5 18.4 %all-to-all-start.4 = ((bf16[128,4,384]{0,2,1:T(8,128)(2,1)}), bf16[128,4,384]{0,2,1:T(8,128)(2,1)S(1)}, u32[]{:S(2)}, u32[]{:S(2)}) async-start(bf16[128,4,384]{0,2,1:T(8,128)(2,1)} %bitcast.14), calls=%async_computation.4 | async-start | bytes 786432 | tf_op jit(solution)/shard_map/all_to_all | solution.py:100
  81.9 2.6 %copy-start.4 = (bf16[512,3,128]{2,0,1:T(8,128)(2,1)S(1)}, bf16[512,3,128]{2,0,1:T(8,128)(2,1)}, u32[]{:S(2)}) copy-start(bf16[512,3,128]{2,0,1:T(8,128)(2,1)} %copy.96) | copy-start | bytes 1179652
  81.9 2.5 %copy-start.6 = (bf16[64,3,128]{2,0,1:T(8,128)(2,1)S(1)}, bf16[64,3,128]{2,0,1:T(8,128)(2,1)}, u32[]{:S(2)}) copy-start(bf16[64,3,128]{2,0,1:T(8,128)(2,1)} %copy.97) | copy-start | bytes 147460
  82.0 4.5 %slice-start = ((s8[4423680]{0:T(1024)(128)(4,1)}), s8[4194304]{0:T(1024)(128)(4,1)S(1)}, s32[]{:S(2)}) async-start(s8[4423680]{0:T(1024)(128)(4,1)} %bitcast.108), calls=%async_computation.12 | async-start | bytes 8388608
  84.5 2.0 slice-start.1
  87.5 1.3 copy-start.11
  87.5 1.3 copy-start.16
  87.5 1.3 copy-start.18
  91.6 14.2 %copy-start = (bf16[4,576,3,128]{3,1,2,0:T(8,128)(2,1)S(1)}, bf16[4,576,3,128]{3,1,2,0:T(8,128)(2,1)}, u32[]{:S(2)}) copy-start(bf16[4,576,3,128]{3,1,2,0:T(8,128)(2,1)} %convert_bitcast_fusion) | copy-start | bytes 5308420
  92.8 10.5 %copy-start.14 = (f32[4,144,3]{1,0,2:T(4,128)S(1)}, f32[4,144,3]{1,0,2:T(4,128)}, u32[]{:S(2)}) copy-start(f32[4,144,3]{1,0,2:T(4,128)} %get-tuple-element.63) | copy-start | bytes 20740
  98.4 10.6 %all-to-all-start.10 = ((bf16[4,16,384]{2,1,0:T(8,128)(2,1)}), bf16[4,16,384]{2,1,0:T(8,128)(2,1)S(1)}, u32[]{:S(2)}, u32[]{:S(2)}) async-start(bf16[4,16,384]{2,1,0:T(8,128)(2,1)} %bitcast.44), calls=%async_computation.10 | async-start | bytes 98304 | tf_op jit(solution)/shard_map/all_to_all | solution.py:155
  109.0 9.2 %copy-start.8 = (bf16[4,16,384]{2,1,0:T(8,128)(2,1)}, bf16[4,16,384]{2,1,0:T(8,128)(2,1)S(1)}, u32[]{:S(2)}) copy-start(bf16[4,16,384]{2,1,0:T(8,128)(2,1)S(1)} %all-to-all-done.10) | copy-start | bytes 147460
  109.0 9.2 %all-to-all-start.11 = ((bf16[4,16,384]{2,1,0:T(8,128)(2,1)}), bf16[4,16,384]{2,1,0:T(8,128)(2,1)S(1)}, u32[]{:S(2)}, u32[]{:S(2)}) async-start(bf16[4,16,384]{2,1,0:T(8,128)(2,1)} %all_to_all.177), calls=%async_computation.11 | async-start | bytes 98304 | tf_op jit(solution)/shard_map/all_to_all | solution.py:156
  112.5 48.3 %copy-start.19 = (f32[128]{0:T(128)S(1)}, f32[128]{0:T(128)}, u32[]{:S(2)}) copy-start(f32[128]{0:T(128)} %get-tuple-element.60) | copy-start | bytes 1540
  112.5 48.3 %copy-start.20 = (f32[128]{0:T(128)S(1)}, f32[128]{0:T(128)}, u32[]{:S(2)}) copy-start(f32[128]{0:T(128)} %get-tuple-element.62) | copy-start | bytes 1540
  118.2 9.1 %all-to-all-start.9 = ((bf16[4,16,384]{2,1,0:T(8,128)(2,1)}), bf16[4,16,384]{2,1,0:T(8,128)(2,1)S(1)}, u32[]{:S(2)}, u32[]{:S(2)}) async-start(bf16[4,16,384]{2,1,0:T(8,128)(2,1)} %copy_bitcast_fusion), calls=%async_computation.9 | async-start | bytes 98304 | tf_op jit(solution)/shard_map/all_to_all | solution.py:154
  121.5 80.1 %copy-start.9 = (bf16[4,16,384]{2,1,0:T(8,128)(2,1)S(1)}, bf16[4,16,384]{2,1,0:T(8,128)(2,1)}, u32[]{:S(2)}) copy-start(bf16[4,16,384]{2,1,0:T(8,128)(2,1)} %copy-done.8) | copy-start | bytes 147460
  127.2 12.3 %all-to-all-start.7 = ((bf16[4,128,384]{2,1,0:T(8,128)(2,1)}), bf16[4,128,384]{2,1,0:T(8,128)(2,1)S(1)}, u32[]{:S(2)}, u32[]{:S(2)}) async-start(bf16[4,128,384]{2,1,0:T(8,128)(2,1)} %bitcast.38), calls=%async_computation.7 | async-start | bytes 786432 | tf_op jit(solution)/shard_map/all_to_all | solution.py:152
  139.6 17.8 %all-to-all-start.8 = ((bf16[4,128,384]{1,2,0:T(8,128)(2,1)}), bf16[4,128,384]{1,2,0:T(8,128)(2,1)S(1)}, u32[]{:S(2)}, u32[]{:S(2)}) async-start(bf16[4,128,384]{1,2,0:T(8,128)(2,1)} %copy.115), calls=%async_computation.8 | async-start | bytes 786432 | tf_op jit(solution)/shard_map/all_to_all | solution.py:153
  157.4 48.3 %all-to-all-start.6 = ((bf16[4,128,384]{1,2,0:T(8,128)(2,1)}), bf16[4,128,384]{1,2,0:T(8,128)(2,1)S(1)}, u32[]{:S(2)}, u32[]{:S(2)}) async-start(bf16[4,128,384]{1,2,0:T(8,128)(2,1)} %bitcast.27), calls=%async_computation.6 | async-start | bytes 786432 | tf_op jit(solution)/shard_map/all_to_all | solution.py:151
  (3 other events, 2.6 us)
where the time goes:
time: 208 us; the launch traced here: 207 us
  waiting for transfers between devices  53.8 us (26%)
  starting transfers between devices  47.8 us (23%)
  blocking collectives  40.7 us (20%)
  local copies, waits for them, and re-layouts  30.2 us (15%)
  other arithmetic  22.3 us (11%)
  matrix products  10.6 us (5%)
    psum x1, blocking collectives, local(): gain_q, gain_k = lax.psum((dq_gain, dk_gain), ('dp', 'seq'))  40.7 us
    unnamed x53, local copies, waits for them, and re-layouts  11.5 us
    all_to_all x1, waiting for transfers between devices, local(): lax.all_to_all(returned[2], 'seq', split_axis=0, concat_axis=1, tiled=True)  11.2 us
    all_to_all x1, waiting for transfers between devices, local(): lax.all_to_all(image_q, 'seq', split_axis=1, concat_axis=0, tiled=True)  8.56 us
    all_to_all x1, waiting for transfers between devices, local(): lax.all_to_all(returned[1], 'seq', split_axis=0, concat_axis=1, tiled=True)  7.73 us
    reduce_sum x1, other arithmetic, group_back(): log_total = jnp.log(jnp.sum(jnp.exp(shifted), axis=-1, keepdims=True))  7 us
    sub x1, other arithmetic, group_back(): shifted = scores - row_max  6.39 us
    all_to_all x1, starting transfers between devices, local(): lax.all_to_all(text_q, 'seq', split_axis=1, concat_axis=0, tiled=True)  6.35 us
  transfers between devices with their start and end apart: 12, of which 10 were waited for; matrix products, arithmetic and copies ran while one was open for 19% of the time, Pallas kernels for 0%

commit v1 on v0

--- a/solution.py
+++ b/solution.py
@@ -5,6 +5,22 @@
 
 HEAD_DIM = 128
 epsilon = 1e-06
+
+
+def swapped_with_each(x, axis, split, join):
+    ways, here = (lax.axis_size(axis), lax.axis_index(axis))
+    width = x.shape[split] // ways
+    lengths = list(x.shape)
+    lengths[split] = width
+    height = lengths[join]
+    lengths[join] = height * ways
+    full = jnp.zeros(lengths, x.dtype)
+    for mask in range(ways):
+        part = lax.dynamic_slice_in_dim(x, (here ^ mask) * width, width, axis=split)
+        if mask:
+            part = lax.ppermute(part, axis, [(d, d ^ mask) for d in range(ways)])
+        full = lax.dynamic_update_slice_in_dim(full, part, (here ^ mask) * height, axis=join)
+    return full
 
 
 def normalize(source, norm_gain):
@@ -149,7 +165,7 @@
     )
     grad_iq, grad_ik, grad_iv, grad_tq, grad_tk, grad_tv = (
         lax.all_to_all(returned[0], "seq", split_axis=0, concat_axis=1, tiled=True),
-        lax.all_to_all(returned[1], "seq", split_axis=0, concat_axis=1, tiled=True),
+        swapped_with_each(returned[1], "seq", 0, 1),
         lax.all_to_all(returned[2], "seq", split_axis=0, concat_axis=1, tiled=True),
         lax.all_to_all(returned[3], "seq", split_axis=0, concat_axis=1, tiled=True),
         lax.all_to_all(returned[4], "seq", split_axis=0, concat_axis=1, tiled=True),

time: 208 us -> 195 us (0.938)
  waiting for transfers between devices: 53.8 us -> 42.3 us
    all_to_all x1 -> x0, waiting for transfers between devices: 7.73 us -> none  [local(): lax.all_to_all(returned[1], 'seq', split_axis=0, concat_axis=1, tiled=True)]
    ppermute x0 -> x3, starting transfers between devices: none -> 4.53 us  [swapped_with_each(): part = lax.ppermute(part, axis, [(d, d ^ mask) for d in range(ways)])]
    all_to_all x1 -> x0, starting transfers between devices: 3.46 us -> none  [local(): lax.all_to_all(returned[1], 'seq', split_axis=0, concat_axis=1, tiled=True)]
    all_to_all x1, waiting for transfers between devices: 11.2 us -> 7.81 us  [local(): lax.all_to_all(returned[2], 'seq', split_axis=0, concat_axis=1, tiled=True)]
    all_to_all x1, starting transfers between devices: 5.59 us -> 3.46 us  [local(): lax.all_to_all(returned[2], 'seq', split_axis=0, concat_axis=1, tiled=True)]
    unnamed x53 -> x54, local copies, waits for them, and re-layouts: 11.5 us -> 10.6 us
  transfers between devices with their start and end apart: 12 -> 14, of which waited for: 10 -> 9; matrix products, arithmetic and copies ran while one was open for 19% -> 20% of each run, Pallas kernels for 0% -> 0%
where the time goes in v1:
time: 195 us; the launch traced here: 194 us
  starting transfers between devices  48.7 us (25%)
  waiting for transfers between devices  42.3 us (22%)
  blocking collectives  40 us (21%)
  local copies, waits for them, and re-layouts  28.5 us (15%)
  other arithmetic  22.3 us (11%)
  matrix products  10.6 us (5%)
    psum x1, blocking collectives, local(): gain_q, gain_k = lax.psum((dq_gain, dk_gain), ('dp', 'seq'))  40 us
    unnamed x54, local copies, waits for them, and re-layouts  10.6 us
    all_to_all x1, waiting for transfers between devices, local(): lax.all_to_all(image_q, 'seq', split_axis=1, concat_axis=0, tiled=True)  8.56 us
    all_to_all x1, waiting for transfers between devices, local(): lax.all_to_all(returned[2], 'seq', split_axis=0, concat_axis=1, tiled=True)  7.81 us
    reduce_sum x1, other arithmetic, group_back(): log_total = jnp.log(jnp.sum(jnp.exp(shifted), axis=-1, keepdims=True))  7 us
    sub x1, other arithmetic, group_back(): shifted = scores - row_max  6.39 us
    all_to_all x1, starting transfers between devices, local(): lax.all_to_all(text_q, 'seq', split_axis=1, concat_axis=0, tiled=True)  6.35 us
    all_to_all x1, starting transfers between devices, local(): lax.all_to_all(returned[0], 'seq', split_axis=0, concat_axis=1, tiled=True)  5.39 us
  transfers between devices with their start and end apart: 14, of which 9 were waited for; matrix products, arithmetic and copies ran while one was open for 20% of the time, Pallas kernels for 0%

profile of v1, /device:TPU:0, one launch (start us, length us, event | category | flops | bytes accessed | tf_op | source)
XLA Modules:
  0.0 193.6 jit_solution(8451381525795501040)
XLA Ops:
  2.2 6.3 %all-to-all-start.2 = ((bf16[16,4,384]{2,0,1:T(8,128)(2,1)}), bf16[16,4,384]{2,0,1:T(8,128)(2,1)S(1)}, u32[]{:S(2)}, u32[]{:S(2)}) async-start(bf16[16,4,384]{2,0,1:T(8,128)(2,1)} %copy.127), calls=%async_computation.2 | async-start | bytes 98304 | tf_op jit(solution)/shard_map/all_to_all | solution.py:117
  9.9 4.3 %all-to-all-done.2 = bf16[16,4,384]{2,0,1:T(8,128)(2,1)S(1)} async-done(((bf16[16,4,384]{2,0,1:T(8,128)(2,1)}), bf16[16,4,384]{2,0,1:T(8,128)(2,1)S(1)}, u32[]{:S(2)}, u32[]{:S(2)}) %all-to-all-start.2) | async-done | bytes 49184 | tf_op jit(solution)/shard_map/all_to_all | solution.py:117
  14.2 3.3 %all-to-all-start.5 = ((bf16[16,4,384]{2,0,1:T(8,128)(2,1)}), bf16[16,4,384]{2,0,1:T(8,128)(2,1)S(1)}, u32[]{:S(2)}, u32[]{:S(2)}) async-start(bf16[16,4,384]{2,0,1:T(8,128)(2,1)} %copy.135), calls=%async_computation.5 | async-start | bytes 98304 | tf_op jit(solution)/shard_map/all_to_all | solution.py:118
  17.5 1.9 copy.122
  19.4 3.8 %all-to-all-done.5 = bf16[16,4,384]{2,0,1:T(8,128)(2,1)S(1)} async-done(((bf16[16,4,384]{2,0,1:T(8,128)(2,1)}), bf16[16,4,384]{2,0,1:T(8,128)(2,1)S(1)}, u32[]{:S(2)}, u32[]{:S(2)}) %all-to-all-start.5) | async-done | bytes 49184 | tf_op jit(solution)/shard_map/all_to_all | solution.py:118
  23.1 3.5 %all-to-all-start = ((bf16[128,4,384]{0,2,1:T(8,128)(2,1)}), bf16[128,4,384]{0,2,1:T(8,128)(2,1)S(1)}, u32[]{:S(2)}, u32[]{:S(2)}) async-start(bf16[128,4,384]{0,2,1:T(8,128)(2,1)} %bitcast), calls=%async_computation | async-start | bytes 786432 | tf_op jit(solution)/shard_map/all_to_all | solution.py:114
  28.3 1.9 copy.126
  30.8 1.9 copy.130
  33.7 2.3 %all-to-all-done = bf16[128,4,384]{0,2,1:T(8,128)(2,1)S(1)} async-done(((bf16[128,4,384]{0,2,1:T(8,128)(2,1)}), bf16[128,4,384]{0,2,1:T(8,128)(2,1)S(1)}, u32[]{:S(2)}, u32[]{:S(2)}) %all-to-all-start) | async-done | bytes 393248 | tf_op jit(solution)/shard_map/all_to_all | solution.py:114
  36.0 3.5 %all-to-all-start.1 = ((bf16[128,4,384]{0,2,1:T(8,128)(2,1)}), bf16[128,4,384]{0,2,1:T(8,128)(2,1)S(1)}, u32[]{:S(2)}, u32[]{:S(2)}) async-start(bf16[128,4,384]{0,2,1:T(8,128)(2,1)} %bitcast.4), calls=%async_computation.1 | async-start | bytes 786432 | tf_op jit(solution)/shard_map/all_to_all | solution.py:113
  40.2 8.6 %all-to-all-done.1 = bf16[128,4,384]{0,2,1:T(8,128)(2,1)S(1)} async-done(((bf16[128,4,384]{0,2,1:T(8,128)(2,1)}), bf16[128,4,384]{0,2,1:T(8,128)(2,1)S(1)}, u32[]{:S(2)}, u32[]{:S(2)}) %all-to-all-start.1) | async-done | bytes 393248 | tf_op jit(solution)/shard_map/all_to_all | solution.py:113
  48.7 3.5 %all-to-all-start.3 = ((bf16[128,4,384]{0,2,1:T(8,128)(2,1)}), bf16[128,4,384]{0,2,1:T(8,128)(2,1)S(1)}, u32[]{:S(2)}, u32[]{:S(2)}) async-start(bf16[128,4,384]{0,2,1:T(8,128)(2,1)} %bitcast.12), calls=%async_computation.3 | async-start | bytes 786432 | tf_op jit(solution)/shard_map/all_to_all | solution.py:115
  54.5 2.9 %fusion.39 = f32[3,576,576]{1,2,0} fusion(bf16[3,128,576]{1,2,0:T(8,128)(2,1)S(1)} %bitcast.117, f32[128]{0:T(128)S(1)} %copy-done.16, f32[576,3]{0,1:T(4,128)S(1)} %fusion.43, bf16[64,3,128]{2,0,1:T(8,128)(2,1)S(1)} %copy.125, bf16[512,3,128]{2,0,1:T(8,128)(2,1)S(1)} %copy.124), kind=kOutput, calls=%fused_computation.58 | convolution fusion | flops 256352256 | bytes 4873472
  57.4 4.1 %all-to-all-done.3 = bf16[128,4,384]{0,2,1:T(8,128)(2,1)S(1)} async-done(((bf16[128,4,384]{0,2,1:T(8,128)(2,1)}), bf16[128,4,384]{0,2,1:T(8,128)(2,1)S(1)}, u32[]{:S(2)}, u32[]{:S(2)}) %all-to-all-start.3) | async-done | bytes 393248 | tf_op jit(solution)/shard_map/all_to_all | solution.py:115
  61.5 3.6 %all-to-all-start.4 = ((bf16[128,4,384]{0,2,1:T(8,128)(2,1)}), bf16[128,4,384]{0,2,1:T(8,128)(2,1)S(1)}, u32[]{:S(2)}, u32[]{:S(2)}) async-start(bf16[128,4,384]{0,2,1:T(8,128)(2,1)} %bitcast.14), calls=%async_computation.4 | async-start | bytes 786432 | tf_op jit(solution)/shard_map/all_to_all | solution.py:116
  65.2 6.4 %bitcast_subtract_fusion = f32[4,3,144,576]{3,2,0,1:T(8,128)} fusion(f32[3,576,4,144]{1,3,2,0:T(8,128)} %bitcast.113), kind=kOutput, calls=%fused_computation.5 | output fusion | flops 2988287 | bytes 7962624 | tf_op jit(solution)/shard_map/while/body/eval_jaxpr/sub | solution.py:46
  73.0 7.0 %fusion.47 = (bf16[4,3,144,576]{3,2,0,1:T(8,128)(2,1)S(1)}, f32[4,3,144,576]{3,2,0,1:T(8,128)}) fusion(f32[4,3,144,576]{3,2,0,1:T(8,128)} %bitcast_subtract_fusion), kind=kOutput, calls=%fused_computation.84 | output fusion | flops 1992959 | bytes 9953280 | tf_op jit(solution)/shard_map/while/body/eval_jaxpr/reduce_sum | solution.py:47
  82.0 2.5 %convert_bitcast_fusion = bf16[4,576,3,128]{3,1,2,0:T(8,128)(2,1)} fusion(bf16[4,3,144,576]{3,2,0,1:T(8,128)(2,1)S(1)} %get-tuple-element.78, bf16[4,16,3,128]{3,1,0,2:T(8,128)(2,1)S(1)} %copy_bitcast_fusion.2, bf16[4,128,3,128]{3,1,0,2:T(8,128)(2,1)S(1)} %copy.136), kind=kOutput, calls=%fused_computation.17 | convolution fusion | flops 256573440 | bytes 4202496 | tf_op jit(solution)/shard_map/while/body/eval_jaxpr/nhqk,nqhd->nkhd/dot_general | solution.py:60
  88.8 2.5 %fusion.26 = (f32[128]{0:T(128)}, f32[4,144,3]{1,0,2:T(4,128)}, f32[4,144,3,128]{3,1,0,2:T(8,128)}) fusion(f32[4,144,3]{1,0,2:T(4,128)S(1)} %copy-done.12, bf16[4,16,3,128]{3,1,0,2:T(8,128)(2,1)S(1)} %copy_bitcast_fusion.3, bf16[4,128,3,128]{3,1,0,2:T(8,128)(2,1)S(1)} %copy.128, f32[128]{0:T(128)S(1)} %copy-done.19, ...), kind=kOutput, calls=%fused_computation.40 | convolution fusion | flops 258562240 | bytes 3782400 | tf_op jit(solution)/shard_map/while/body/eval_jaxpr/nhqk,khd->nqhd/dot_general | solution.py:58
  98.1 4.9 %all-to-all-start.9 = ((bf16[4,16,384]{2,1,0:T(8,128)(2,1)}), bf16[4,16,384]{2,1,0:T(8,128)(2,1)S(1)}, u32[]{:S(2)}, u32[]{:S(2)}) async-start(bf16[4,16,384]{2,1,0:T(8,128)(2,1)} %bitcast.44), calls=%async_computation.9 | async-start | bytes 98304 | tf_op jit(solution)/shard_map/all_to_all | solution.py:171
  103.7 1.7 fusion.31
  106.7 2.0 %all-to-all-done.9 = bf16[4,16,384]{2,1,0:T(8,128)(2,1)S(1)} async-done(((bf16[4,16,384]{2,1,0:T(8,128)(2,1)}), bf16[4,16,384]{2,1,0:T(8,128)(2,1)S(1)}, u32[]{:S(2)}, u32[]{:S(2)}) %all-to-all-start.9) | async-done | bytes 49184 | tf_op jit(solution)/shard_map/all_to_all | solution.py:171
  108.7 3.3 %all-to-all-start.10 = ((bf16[4,16,384]{2,1,0:T(8,128)(2,1)}), bf16[4,16,384]{2,1,0:T(8,128)(2,1)S(1)}, u32[]{:S(2)}, u32[]{:S(2)}) async-start(bf16[4,16,384]{2,1,0:T(8,128)(2,1)} %all_to_all.162), calls=%async_computation.10 | async-start | bytes 98304 | tf_op jit(solution)/shard_map/all_to_all | solution.py:172
  112.6 5.0 %all-to-all-done.10 = bf16[4,16,384]{2,1,0:T(8,128)(2,1)S(1)} async-done(((bf16[4,16,384]{2,1,0:T(8,128)(2,1)}), bf16[4,16,384]{2,1,0:T(8,128)(2,1)S(1)}, u32[]{:S(2)}, u32[]{:S(2)}) %all-to-all-start.10) | async-done | bytes 49184 | tf_op jit(solution)/shard_map/all_to_all | solution.py:172
  117.7 3.5 %all-to-all-start.8 = ((bf16[4,16,384]{2,1,0:T(8,128)(2,1)}), bf16[4,16,384]{2,1,0:T(8,128)(2,1)S(1)}, u32[]{:S(2)}, u32[]{:S(2)}) async-start(bf16[4,16,384]{2,1,0:T(8,128)(2,1)} %copy_bitcast_fusion.1), calls=%async_computation.8 | async-start | bytes 98304 | tf_op jit(solution)/shard_map/all_to_all | solution.py:170
  122.3 4.4 %all-to-all-done.8 = bf16[4,16,384]{2,1,0:T(8,128)(2,1)S(1)} async-done(((bf16[4,16,384]{2,1,0:T(8,128)(2,1)}), bf16[4,16,384]{2,1,0:T(8,128)(2,1)S(1)}, u32[]{:S(2)}, u32[]{:S(2)}) %all-to-all-start.8) | async-done | bytes 49184 | tf_op jit(solution)/shard_map/all_to_all | solution.py:170
  126.7 3.5 %all-to-all-start.7 = ((bf16[4,128,384]{1,2,0:T(8,128)(2,1)}), bf16[4,128,384]{1,2,0:T(8,128)(2,1)S(1)}, u32[]{:S(2)}, u32[]{:S(2)}) async-start(bf16[4,128,384]{1,2,0:T(8,128)(2,1)} %copy.152), calls=%async_computation.7 | async-start | bytes 786432 | tf_op jit(solution)/shard_map/all_to_all | solution.py:169
  131.2 7.8 %all-to-all-done.7 = bf16[4,128,384]{1,2,0:T(8,128)(2,1)S(1)} async-done(((bf16[4,128,384]{1,2,0:T(8,128)(2,1)}), bf16[4,128,384]{1,2,0:T(8,128)(2,1)S(1)}, u32[]{:S(2)}, u32[]{:S(2)}) %all-to-all-start.7) | async-done | bytes 393248 | tf_op jit(solution)/shard_map/all_to_all | solution.py:169
  139.0 5.4 %all-to-all-start.6 = ((bf16[4,128,384]{1,2,0:T(8,128)(2,1)}), bf16[4,128,384]{1,2,0:T(8,128)(2,1)S(1)}, u32[]{:S(2)}, u32[]{:S(2)}) async-start(bf16[4,128,384]{1,2,0:T(8,128)(2,1)} %bitcast.27), calls=%async_computation.6 | async-start | bytes 786432 | tf_op jit(solution)/shard_map/all_to_all | solution.py:167
  144.6 2.1 %collective-permute-start = (bf16[128,384]{0,1:T(8,128)(2,1)S(1)}, bf16[128,384]{0,1:T(8,128)(2,1)S(1)}, u32[]{:S(2)}, u32[]{:S(2)}) collective-permute-start(bf16[128,384]{0,1:T(8,128)(2,1)S(1)} %get-tuple-element.76), channel_id=1, source_target_pairs={{0,1},{1,0},{2,3},{3,2},{4,5},{5,4},{6,7},{7,6},{8,9},{9,8},{10,11... | collective-permute-start | bytes 294920 | tf_op jit(solution)/shard_map/ppermute | solution.py:21
  146.7 2.4 %collective-permute-start.1 = (bf16[128,384]{0,1:T(8,128)(2,1)S(1)}, bf16[128,384]{0,1:T(8,128)(2,1)S(1)}, u32[]{:S(2)}, u32[]{:S(2)}) collective-permute-start(bf16[128,384]{0,1:T(8,128)(2,1)S(1)} %get-tuple-element.75), channel_id=1, source_target_pairs={{0,2},{1,3},{2,0},{3,1},{4,6},{5,7},{6,4},{7,5},{8,10},{9,11},{10,... | collective-permute-start | bytes 294920 | tf_op jit(solution)/shard_map/ppermute | solution.py:21
  149.2 40.0 %all-reduce = (f32[128]{0:T(128)}, f32[128]{0:T(128)}) all-reduce(f32[128]{0:T(128)S(1)} %copy-done.21, f32[128]{0:T(128)S(1)} %copy-done.20), channel_id=1, replica_groups=mesh['dp'=8,'seq'=4] {'dp','seq'}, use_global_device_ids=true, to_apply=%region_10.11 | all-reduce | flops 256 | bytes 2048 | tf_op jit(solution)/shard_map/psum | solution.py:174
  (127 shorter events, 32.7 us)
Async XLA Ops:
  0.6 32.1 %copy-start.7 = (bf16[1,128,1536]{2,1,0:T(8,128)(2,1)S(1)}, bf16[1,128,1536]{2,1,0:T(8,128)(2,1)}, u32[]{:S(2)}) copy-start(bf16[1,128,1536]{2,1,0:T(8,128)(2,1)} %param.13) | copy-start | bytes 1179652
  0.6 38.8 %copy-start.16 = (f32[128]{0:T(128)S(1)}, f32[128]{0:T(128)}, u32[]{:S(2)}) copy-start(f32[128]{0:T(128)} %param.19) | copy-start | bytes 1540
  2.2 12.0 %all-to-all-start.2 = ((bf16[16,4,384]{2,0,1:T(8,128)(2,1)}), bf16[16,4,384]{2,0,1:T(8,128)(2,1)S(1)}, u32[]{:S(2)}, u32[]{:S(2)}) async-start(bf16[16,4,384]{2,0,1:T(8,128)(2,1)} %copy.127), calls=%async_computation.2 | async-start | bytes 98304 | tf_op jit(solution)/shard_map/all_to_all | solution.py:117
  14.2 8.9 %all-to-all-start.5 = ((bf16[16,4,384]{2,0,1:T(8,128)(2,1)}), bf16[16,4,384]{2,0,1:T(8,128)(2,1)S(1)}, u32[]{:S(2)}, u32[]{:S(2)}) async-start(bf16[16,4,384]{2,0,1:T(8,128)(2,1)} %copy.135), calls=%async_computation.5 | async-start | bytes 98304 | tf_op jit(solution)/shard_map/all_to_all | solution.py:118
  23.1 12.8 %all-to-all-start = ((bf16[128,4,384]{0,2,1:T(8,128)(2,1)}), bf16[128,4,384]{0,2,1:T(8,128)(2,1)S(1)}, u32[]{:S(2)}, u32[]{:S(2)}) async-start(bf16[128,4,384]{0,2,1:T(8,128)(2,1)} %bitcast), calls=%async_computation | async-start | bytes 786432 | tf_op jit(solution)/shard_map/all_to_all | solution.py:114
  27.5 25.9 %copy-start.18 = (f32[128]{0:T(128)S(1)}, f32[128]{0:T(128)}, u32[]{:S(2)}) copy-start(f32[128]{0:T(128)} %param.18) | copy-start | bytes 1540
  36.0 16.3 %copy-start.3 = (bf16[128,4,384]{0,2,1:T(8,128)(2,1)}, bf16[128,4,384]{0,2,1:T(8,128)(2,1)S(1)}, u32[]{:S(2)}) copy-start(bf16[128,4,384]{0,2,1:T(8,128)(2,1)S(1)} %all-to-all-done) | copy-start | bytes 1179652
  36.0 12.8 %all-to-all-start.1 = ((bf16[128,4,384]{0,2,1:T(8,128)(2,1)}), bf16[128,4,384]{0,2,1:T(8,128)(2,1)S(1)}, u32[]{:S(2)}, u32[]{:S(2)}) async-start(bf16[128,4,384]{0,2,1:T(8,128)(2,1)} %bitcast.4), calls=%async_computation.1 | async-start | bytes 786432 | tf_op jit(solution)/shard_map/all_to_all | solution.py:113
  48.7 12.8 %all-to-all-start.3 = ((bf16[128,4,384]{0,2,1:T(8,128)(2,1)}), bf16[128,4,384]{0,2,1:T(8,128)(2,1)S(1)}, u32[]{:S(2)}, u32[]{:S(2)}) async-start(bf16[128,4,384]{0,2,1:T(8,128)(2,1)} %bitcast.12), calls=%async_computation.3 | async-start | bytes 786432 | tf_op jit(solution)/shard_map/all_to_all | solution.py:115
  53.0 18.6 %copy-start.13 = (f32[4,144,3]{1,0,2:T(4,128)}, f32[4,144,3]{1,0,2:T(4,128)S(1)}, u32[]{:S(2)}) copy-start(f32[4,144,3]{1,0,2:T(4,128)S(1)} %fusion.32) | copy-start | bytes 20740
  53.0 18.6 %copy-start.11 = (f32[4,144,3]{1,0,2:T(4,128)}, f32[4,144,3]{1,0,2:T(4,128)S(1)}, u32[]{:S(2)}) copy-start(f32[4,144,3]{1,0,2:T(4,128)S(1)} %fusion.42) | copy-start | bytes 20740
  53.4 18.2 %copy-start.14 = (f32[576,3]{0,1:T(4,128)}, f32[576,3]{0,1:T(4,128)S(1)}, u32[]{:S(2)}) copy-start(f32[576,3]{0,1:T(4,128)S(1)} %fusion.29) | copy-start | bytes 20740
  61.5 18.5 %all-to-all-start.4 = ((bf16[128,4,384]{0,2,1:T(8,128)(2,1)}), bf16[128,4,384]{0,2,1:T(8,128)(2,1)S(1)}, u32[]{:S(2)}, u32[]{:S(2)}) async-start(bf16[128,4,384]{0,2,1:T(8,128)(2,1)} %bitcast.14), calls=%async_computation.4 | async-start | bytes 786432 | tf_op jit(solution)/shard_map/all_to_all | solution.py:116
  81.9 2.6 %copy-start.4 = (bf16[512,3,128]{2,0,1:T(8,128)(2,1)S(1)}, bf16[512,3,128]{2,0,1:T(8,128)(2,1)}, u32[]{:S(2)}) copy-start(bf16[512,3,128]{2,0,1:T(8,128)(2,1)} %copy.132) | copy-start | bytes 1179652
  81.9 2.6 %copy-start.6 = (bf16[64,3,128]{2,0,1:T(8,128)(2,1)S(1)}, bf16[64,3,128]{2,0,1:T(8,128)(2,1)}, u32[]{:S(2)}) copy-start(bf16[64,3,128]{2,0,1:T(8,128)(2,1)} %copy.133) | copy-start | bytes 147460
  82.0 4.5 %slice-start = ((s8[4423680]{0:T(1024)(128)(4,1)}), s8[4194304]{0:T(1024)(128)(4,1)S(1)}, s32[]{:S(2)}) async-start(s8[4423680]{0:T(1024)(128)(4,1)} %bitcast.114), calls=%async_computation.11 | async-start | bytes 8388608
  84.5 2.0 %slice-start.1 = ((s8[4423680]{0:T(1024)(128)(4,1)}), s8[229376]{0:T(1024)(128)(4,1)S(1)}, s32[]{:S(2)}) async-start(s8[4423680]{0:T(1024)(128)(4,1)} %bitcast.114), calls=%async_computation.12 | async-start | bytes 458752
  91.6 13.8 %copy-start = (bf16[4,576,3,128]{3,1,2,0:T(8,128)(2,1)S(1)}, bf16[4,576,3,128]{3,1,2,0:T(8,128)(2,1)}, u32[]{:S(2)}) copy-start(bf16[4,576,3,128]{3,1,2,0:T(8,128)(2,1)} %convert_bitcast_fusion) | copy-start | bytes 5308420
  92.8 10.2 %copy-start.15 = (f32[4,144,3]{1,0,2:T(4,128)S(1)}, f32[4,144,3]{1,0,2:T(4,128)}, u32[]{:S(2)}) copy-start(f32[4,144,3]{1,0,2:T(4,128)} %get-tuple-element.71) | copy-start | bytes 20740
  98.1 10.6 %all-to-all-start.9 = ((bf16[4,16,384]{2,1,0:T(8,128)(2,1)}), bf16[4,16,384]{2,1,0:T(8,128)(2,1)S(1)}, u32[]{:S(2)}, u32[]{:S(2)}) async-start(bf16[4,16,384]{2,1,0:T(8,128)(2,1)} %bitcast.44), calls=%async_computation.9 | async-start | bytes 98304 | tf_op jit(solution)/shard_map/all_to_all | solution.py:171
  108.7 9.0 %copy-start.9 = (bf16[4,16,384]{2,1,0:T(8,128)(2,1)}, bf16[4,16,384]{2,1,0:T(8,128)(2,1)S(1)}, u32[]{:S(2)}) copy-start(bf16[4,16,384]{2,1,0:T(8,128)(2,1)S(1)} %all-to-all-done.9) | copy-start | bytes 147460
  108.7 8.9 %all-to-all-start.10 = ((bf16[4,16,384]{2,1,0:T(8,128)(2,1)}), bf16[4,16,384]{2,1,0:T(8,128)(2,1)S(1)}, u32[]{:S(2)}, u32[]{:S(2)}) async-start(bf16[4,16,384]{2,1,0:T(8,128)(2,1)} %all_to_all.162), calls=%async_computation.10 | async-start | bytes 98304 | tf_op jit(solution)/shard_map/all_to_all | solution.py:172
  112.6 36.6 %copy-start.20 = (f32[128]{0:T(128)S(1)}, f32[128]{0:T(128)}, u32[]{:S(2)}) copy-start(f32[128]{0:T(128)} %get-tuple-element.68) | copy-start | bytes 1540
  112.6 36.6 %copy-start.21 = (f32[128]{0:T(128)S(1)}, f32[128]{0:T(128)}, u32[]{:S(2)}) copy-start(f32[128]{0:T(128)} %get-tuple-element.70) | copy-start | bytes 1540
  117.7 9.1 %all-to-all-start.8 = ((bf16[4,16,384]{2,1,0:T(8,128)(2,1)}), bf16[4,16,384]{2,1,0:T(8,128)(2,1)S(1)}, u32[]{:S(2)}, u32[]{:S(2)}) async-start(bf16[4,16,384]{2,1,0:T(8,128)(2,1)} %copy_bitcast_fusion.1), calls=%async_computation.8 | async-start | bytes 98304 | tf_op jit(solution)/shard_map/all_to_all | solution.py:170
  121.2 68.1 %copy-start.10 = (bf16[4,16,384]{2,1,0:T(8,128)(2,1)S(1)}, bf16[4,16,384]{2,1,0:T(8,128)(2,1)}, u32[]{:S(2)}) copy-start(bf16[4,16,384]{2,1,0:T(8,128)(2,1)} %copy-done.9) | copy-start | bytes 147460
  126.7 12.3 %all-to-all-start.7 = ((bf16[4,128,384]{1,2,0:T(8,128)(2,1)}), bf16[4,128,384]{1,2,0:T(8,128)(2,1)S(1)}, u32[]{:S(2)}, u32[]{:S(2)}) async-start(bf16[4,128,384]{1,2,0:T(8,128)(2,1)} %copy.152), calls=%async_computation.7 | async-start | bytes 786432 | tf_op jit(solution)/shard_map/all_to_all | solution.py:169
  139.0 53.7 %all-to-all-start.6 = ((bf16[4,128,384]{1,2,0:T(8,128)(2,1)}), bf16[4,128,384]{1,2,0:T(8,128)(2,1)S(1)}, u32[]{:S(2)}, u32[]{:S(2)}) async-start(bf16[4,128,384]{1,2,0:T(8,128)(2,1)} %bitcast.27), calls=%async_computation.6 | async-start | bytes 786432 | tf_op jit(solution)/shard_map/all_to_all | solution.py:167
  144.6 46.6 %collective-permute-start = (bf16[128,384]{0,1:T(8,128)(2,1)S(1)}, bf16[128,384]{0,1:T(8,128)(2,1)S(1)}, u32[]{:S(2)}, u32[]{:S(2)}) collective-permute-start(bf16[128,384]{0,1:T(8,128)(2,1)S(1)} %get-tuple-element.76), channel_id=1, source_target_pairs={{0,1},{1,0},{2,3},{3,2},{4,5},{5,4},{6,7},{7,6},{8,9},{9,8},{10,11... | collective-permute-start | bytes 294920 | tf_op jit(solution)/shard_map/ppermute | solution.py:21
  146.7 44.7 %collective-permute-start.1 = (bf16[128,384]{0,1:T(8,128)(2,1)S(1)}, bf16[128,384]{0,1:T(8,128)(2,1)S(1)}, u32[]{:S(2)}, u32[]{:S(2)}) collective-permute-start(bf16[128,384]{0,1:T(8,128)(2,1)S(1)} %get-tuple-element.75), channel_id=1, source_target_pairs={{0,2},{1,3},{2,0},{3,1},{4,6},{5,7},{6,4},{7,5},{8,10},{9,11},{10,... | collective-permute-start | bytes 294920 | tf_op jit(solution)/shard_map/ppermute | solution.py:21
  149.1 42.5 %collective-permute-start.2 = (bf16[128,384]{0,1:T(8,128)(2,1)S(1)}, bf16[128,384]{0,1:T(8,128)(2,1)S(1)}, u32[]{:S(2)}, u32[]{:S(2)}) collective-permute-start(bf16[128,384]{0,1:T(8,128)(2,1)S(1)} %get-tuple-element.74), channel_id=1, source_target_pairs={{0,3},{1,2},{2,1},{3,0},{4,7},{5,6},{6,5},{7,4},{8,11},{9,10},{10,... | collective-permute-start | bytes 294920 | tf_op jit(solution)/shard_map/ppermute | solution.py:21
  191.8 1.9 copy-start.8
  (6 other events, 6.4 us)
